TPU v7x, 256 devices: a whole 4x4x8 slice. The times are simulated.
256 devices in a mesh: row: 8 (over y_hi, x), col: 32 (over z, y_lo, core).
Axes of the slice: x: 4, y: 4 (y_hi: 2, y_lo: 2; y = y_hi * 2 + y_lo), z: 8, core: 2. Of those that a mesh axis runs over, the one named last changes fastest.
Arguments:
- legendre: bfloat16 [512, 512, 512], P('row', 'col'), may hold values from -6 to 6
- vectors: bfloat16 [512, 512, 256], P('row', 'col'), may hold values from -6 to 6
- panel_orders: int32 [8], replicated, may hold values from 0 to 511, as said below
- cycle_span: int32 [512, 2], replicated, may hold values from 0 to 2047, as said below
- cycle_weight: float32 [512], replicated, may hold values from 0.0009765625 to 0.0029296875
Outputs:
- projected: bfloat16 [512, 8, 256], P('col', 'row')
Inputs may be any that keep to these rules, and one draw needn't show every extreme that they name: `panel_orders`: the 8 entries are distinct orders; 0 and 511 are among them. `cycle_span`: in every cycle the first entry is smaller than the second.
All inputs are finite; a program needn't handle non-finite values.
Results may differ from a plain program's by a relative error of at most 0.008.
Values may be sent and summed in bfloat16 or wider, within the bound.
No kernel may reach another device: no remote copies, remote signals or barrier semaphores. Data moves between devices by JAX's collectives and lax.ppermute only.
A program may use at most 64 MiB of HBM per device.

v0:
```python
import math
import jax
import jax.numpy as jnp
from jax import lax
from jax.sharding import PartitionSpec as P

NPHI = 2048


def from_everyone(array, axis):
    copies = jnp.broadcast_to(array, (lax.axis_size(axis), *array.shape))
    return lax.all_to_all(copies, axis, split_axis=0, concat_axis=0, tiled=True)


def taken_together(array, axis):
    return from_everyone(array, axis).astype(jnp.float32).sum(axis=0)


def split_up(array, dim, length):
    before, after = (array.shape[:dim], array.shape[dim + 1 :])
    return jnp.moveaxis(array.reshape(*before, length, -1, *after), dim, 0)


def summed_on_arrival(array, axis, dim):
    length = lax.axis_size(axis)
    pieces = lax.all_to_all(split_up(array, dim, length), axis, 0, 0, tiled=True)
    return jnp.sum(pieces.astype(jnp.float32), axis=0)


def mask_coef(wavenumber, span_start, span_stop):
    cell_angle = 2.0 * math.pi / NPHI
    upper_sine = jnp.sin(cell_angle * (wavenumber * span_stop % NPHI).astype(jnp.float32))
    lower_sine = jnp.sin(cell_angle * (wavenumber * span_start % NPHI).astype(jnp.float32))
    half_angle = 2.0 * jnp.sin(math.pi / NPHI * wavenumber.astype(jnp.float32))
    safe_denom = jnp.where(wavenumber == 0, jnp.ones_like(half_angle), half_angle)
    span_width = cell_angle * (span_stop - span_start).astype(jnp.float32)
    return jnp.where(
        wavenumber == 0, span_width, cell_angle * (upper_sine - lower_sine) / safe_denom
    )


def cycle_mix(first_orders, col_orders, cycle_span, cycle_weight):
    span_start = cycle_span[:, 0][None, None, :]
    span_stop = cycle_span[:, 1][None, None, :]
    order_gap = jnp.abs(first_orders[:, None] - col_orders[None, :])[:, :, None]
    order_sum = (first_orders[:, None] + col_orders[None, :])[:, :, None]
    coef_sum = mask_coef(order_gap, span_start, span_stop) + mask_coef(
        order_sum, span_start, span_stop
    )
    return 0.5 * cycle_weight[None, None, :] * coef_sum


def per_device(legendre, vectors, panel_orders, cycle_span, cycle_weight):
    ord_count, deg_count, cycle_count = legendre.shape
    vec_count = vectors.shape[2]
    panel_count = panel_orders.shape[0]
    first_order = lax.axis_index("row") * ord_count
    first_degree = lax.axis_index("col") * deg_count
    local_orders = first_order + jnp.arange(ord_count, dtype=jnp.int32)
    local_degrees = first_degree + jnp.arange(deg_count, dtype=jnp.int32)
    keep_mask = local_degrees[None, :] >= local_orders[:, None]
    tables = jnp.where(keep_mask[:, :, None], legendre, jnp.zeros((), jnp.bfloat16))
    picker = (panel_orders[:, None] == local_orders[None, :]).astype(jnp.bfloat16)
    owned_terms = jnp.einsum("pi,ilj->plj", picker, legendre, preferred_element_type=jnp.float32)
    panel_keep = local_degrees[None, :] >= panel_orders[:, None]
    owned_terms = jnp.where(panel_keep[:, :, None], owned_terms, 0.0)
    summed = (
        taken_together(owned_terms.astype(jnp.bfloat16), "row")
        .astype(jnp.float32)
        .astype(jnp.bfloat16)
    )
    panel_rows = lax.all_gather(summed, "col", axis=1, tiled=True)
    mix_coef = cycle_mix(panel_orders, local_orders, cycle_span, cycle_weight)
    order_block = 8

    def add_block(block_index, running):
        block_start = block_index * order_block
        active = first_order + block_start <= first_degree + deg_count - 1

        def add_terms(partial_value):
            col_tables = lax.dynamic_slice_in_dim(tables, block_start, order_block, 0)
            cycle_coef = lax.dynamic_slice_in_dim(mix_coef, block_start, order_block, 1)
            vec_block = lax.dynamic_slice_in_dim(vectors, block_start, order_block, 0)
            vec_block = vec_block.reshape(order_block * deg_count, vec_count)
            weighted = (cycle_coef[:, :, None, :] * col_tables[None]).astype(jnp.bfloat16)
            weighted = weighted.reshape(panel_count, order_block * deg_count, cycle_count)
            panel_block = jnp.einsum(
                "plj,pqj->plq", panel_rows, weighted, preferred_element_type=jnp.float32
            )
            panel_block = panel_block.astype(jnp.bfloat16)
            return partial_value + jnp.einsum(
                "plq,qk->lpk", panel_block, vec_block, preferred_element_type=jnp.float32
            )

        def keep_terms(partial_value):
            return partial_value

        return lax.cond(active, add_terms, keep_terms, running)

    initial = jnp.zeros((panel_rows.shape[1], panel_count, vec_count), jnp.float32)
    whole_terms = lax.fori_loop(0, ord_count // order_block, add_block, initial)
    by_panel = summed_on_arrival(whole_terms.astype(jnp.bfloat16), "row", 1)
    result = summed_on_arrival(by_panel.astype(jnp.bfloat16), "col", 0)
    return result.astype(jnp.bfloat16)


def solution(mesh):
    in_specs = (P("row", "col", None), P("row", "col", None), P(), P(), P())
    out_specs = P("col", "row", None)
    return jax.shard_map(
        per_device, mesh=mesh, in_specs=in_specs, out_specs=out_specs, check_vma=False
    )
```

profile of v0, /device:TPU:1, one launch (start us, length us, event | category | flops | bytes accessed | tf_op | source)
XLA Modules:
  0.0 399.3 jit_solution(15246112433112409109)
XLA Ops:
  6.6 0.8 broadcast_compare_fusion.1
  7.4 2.5 fusion.20
  9.9 0.1 broadcast_in_dim.79
  10.0 23.6 %all_to_all.15 = bf16[8,8,16,512]{3,2,1,0:T(8,128)(2,1)S(1)} all-to-all(bf16[8,8,16,512]{3,2,1,0:T(8,128)(2,1)S(1)} %broadcast_in_dim.79), channel_id=1, replica_groups=mesh['row'=8,'col'=32] {'row'}, dimensions={0} | all-to-all | bytes 2097152 | tf_op jit(solution)/shard_map/all_to_all | solution.py:12
  33.7 0.8 reduce_sum.38
  34.8 0.1 multiply_select_fusion.4
  34.9 1.3 broadcast_select_fusion
  36.2 65.4 %all-gather.2.cloned.1.call-done = bf16[8,512,512]{2,1,0:T(8,128)(2,1)} async-done(((bf16[8,16,512]{2,1,0:T(8,128)(2,1)}), bf16[8,512,512]{2,1,0:T(8,128)(2,1)}) %all-gather.2.cloned.1.call-update) | async-done | bytes 4194320 | tf_op jit(solution)/shard_map/all_gather | solution.py:72
  101.6 2.5 broadcast_in_dim.71
  104.1 133.4 %while.19 = (s32[]{:T(128)}, f32[512,8,256]{0,2,1:T(8,128)}, s32[]{:T(128)}, s32[]{:T(128)}, bf16[64,16,256]{2,1,0:T(8,128)(2,1)}, /*index=5*/bf16[64,16,512]{2,...) while((s32[]{:T(128)}, f32[512,8,256]{0,2,1:T(8,128)}, ...), condition=%wide.region_4.5_spmd.clone, body=%wide.region_1.4_spmd.clone.sunk | while | flops 823001088 | bytes 32586012 | solution.py:101
  104.1 1.1 broadcast_in_dim.105
  105.2 2.8 fusion.32
  108.0 0.1 broadcast.279
  108.1 25.3 %conditional.3 = (f32[512,8,256]{0,2,1:T(8,128)}) conditional(s32[]{:T(128)} %convert_element_type.117, f32[512,8,256]{0,2,1:T(8,128)} %get-tuple-element.557, (s32[]{:T(128)}, bf16[64,16,256]{2,1,0:T(8,128)(2,1)}, f32[512]{0:T(512)S(1)}, bf16[64,16,512]{2,1,0:T(8,128)(2,1)}, bf16[8,512,512]{2,1,0:T(8,128)(2,1)}, ...), branch_computations={%region_2.2_spmd, %region_3.3_spmd.clone} | conditional | flops 809369600 | bytes 26283966 | solution.py:98
  108.3 0.8 constant_dynamic-slice_fusion.5
  109.2 0.9 constant_dynamic-slice_fusion.3
  110.1 14.6 %multiply_sine_fusion.3 = (f32[8,64,512]{2,1,0:T(8,128)S(1)}, f32[8,64,512]{2,1,0:T(8,128)S(1)}, f32[8,64,512]{2,1,0:T(8,128)S(1)}, f32[8,64,512]{2,1,0:T(8,128)S(1)}) fusion(f32[8,64,512]{2,1,0:T(8,128)S(1)} %get-tuple-element.343, f32[8,64,512]{2,1,0:T(8,128)S(1)} %get-tuple-element.344, f32[8,64,512]{2,1,0:T(8,128)} %get-tuple-element.349, ...), kind=kLoop, calls=%fused_computation.9 | loop fusion | flops 1048576 | bytes 9437184 | tf_op jit(solution)/shard_map/sin | solution.py:32
  124.7 1.0 fusion.8
  125.8 0.2 fusion.2
  125.9 7.5 %bitcast_add_fusion = f32[512,8,256]{0,2,1:T(8,128)} fusion(f32[512,8,256]{0,2,1:T(8,128)} %get-tuple-element.329, bf16[128,256,1]{1,0,2:T(8,128)(2,1)S(1)} %bitcast.39, bf16[8,128,512]{2,1,0:T(8,128)(2,1)S(1)} %fusion.2, bf16[8,512,512]{2,1,0:T(8,128)(2,1)} %get-tuple-element.333), kind=kOutput, calls=%fused_computation.1 | convolution fusion | flops 806879232 | bytes 13697024 | tf_op jit(solution)/shard_map/while/body/eval_jaxpr/cond/branch_1_fun/plq,qk->lpk/dot_general | solution.py:91
  133.4 1.1 broadcast_in_dim.105
  134.5 2.8 fusion.32
  137.3 0.1 broadcast.279
  137.4 25.3 %conditional.3 = (f32[512,8,256]{0,2,1:T(8,128)}) conditional(s32[]{:T(128)} %convert_element_type.117, f32[512,8,256]{0,2,1:T(8,128)} %get-tuple-element.557, (s32[]{:T(128)}, bf16[64,16,256]{2,1,0:T(8,128)(2,1)}, f32[512]{0:T(512)S(1)}, bf16[64,16,512]{2,1,0:T(8,128)(2,1)}, bf16[8,512,512]{2,1,0:T(8,128)(2,1)}, ...), branch_computations={%region_2.2_spmd, %region_3.3_spmd.clone} | conditional | flops 809369600 | bytes 26283966 | solution.py:98
  137.6 0.8 constant_dynamic-slice_fusion.5
  138.4 0.9 constant_dynamic-slice_fusion.3
  139.4 14.6 %multiply_sine_fusion.3 = (f32[8,64,512]{2,1,0:T(8,128)S(1)}, f32[8,64,512]{2,1,0:T(8,128)S(1)}, f32[8,64,512]{2,1,0:T(8,128)S(1)}, f32[8,64,512]{2,1,0:T(8,128)S(1)}) fusion(f32[8,64,512]{2,1,0:T(8,128)S(1)} %get-tuple-element.343, f32[8,64,512]{2,1,0:T(8,128)S(1)} %get-tuple-element.344, f32[8,64,512]{2,1,0:T(8,128)} %get-tuple-element.349, ...), kind=kLoop, calls=%fused_computation.9 | loop fusion | flops 1048576 | bytes 9437184 | tf_op jit(solution)/shard_map/sin | solution.py:32
  154.0 1.0 fusion.8
  155.0 0.2 fusion.2
  155.2 7.5 %bitcast_add_fusion = f32[512,8,256]{0,2,1:T(8,128)} fusion(f32[512,8,256]{0,2,1:T(8,128)} %get-tuple-element.329, bf16[128,256,1]{1,0,2:T(8,128)(2,1)S(1)} %bitcast.39, bf16[8,128,512]{2,1,0:T(8,128)(2,1)S(1)} %fusion.2, bf16[8,512,512]{2,1,0:T(8,128)(2,1)} %get-tuple-element.333), kind=kOutput, calls=%fused_computation.1 | convolution fusion | flops 806879232 | bytes 13697024 | tf_op jit(solution)/shard_map/while/body/eval_jaxpr/cond/branch_1_fun/plq,qk->lpk/dot_general | solution.py:91
  162.7 1.1 broadcast_in_dim.105
  163.8 2.8 fusion.32
  166.6 0.1 broadcast.279
  166.7 25.3 %conditional.3 = (f32[512,8,256]{0,2,1:T(8,128)}) conditional(s32[]{:T(128)} %convert_element_type.117, f32[512,8,256]{0,2,1:T(8,128)} %get-tuple-element.557, (s32[]{:T(128)}, bf16[64,16,256]{2,1,0:T(8,128)(2,1)}, f32[512]{0:T(512)S(1)}, bf16[64,16,512]{2,1,0:T(8,128)(2,1)}, bf16[8,512,512]{2,1,0:T(8,128)(2,1)}, ...), branch_computations={%region_2.2_spmd, %region_3.3_spmd.clone} | conditional | flops 809369600 | bytes 26283966 | solution.py:98
  166.9 0.8 constant_dynamic-slice_fusion.5
  167.7 0.9 constant_dynamic-slice_fusion.3
  168.7 14.6 %multiply_sine_fusion.3 = (f32[8,64,512]{2,1,0:T(8,128)S(1)}, f32[8,64,512]{2,1,0:T(8,128)S(1)}, f32[8,64,512]{2,1,0:T(8,128)S(1)}, f32[8,64,512]{2,1,0:T(8,128)S(1)}) fusion(f32[8,64,512]{2,1,0:T(8,128)S(1)} %get-tuple-element.343, f32[8,64,512]{2,1,0:T(8,128)S(1)} %get-tuple-element.344, f32[8,64,512]{2,1,0:T(8,128)} %get-tuple-element.349, ...), kind=kLoop, calls=%fused_computation.9 | loop fusion | flops 1048576 | bytes 9437184 | tf_op jit(solution)/shard_map/sin | solution.py:32
  183.3 1.0 fusion.8
  184.3 0.2 fusion.2
  184.5 7.5 %bitcast_add_fusion = f32[512,8,256]{0,2,1:T(8,128)} fusion(f32[512,8,256]{0,2,1:T(8,128)} %get-tuple-element.329, bf16[128,256,1]{1,0,2:T(8,128)(2,1)S(1)} %bitcast.39, bf16[8,128,512]{2,1,0:T(8,128)(2,1)S(1)} %fusion.2, bf16[8,512,512]{2,1,0:T(8,128)(2,1)} %get-tuple-element.333), kind=kOutput, calls=%fused_computation.1 | convolution fusion | flops 806879232 | bytes 13697024 | tf_op jit(solution)/shard_map/while/body/eval_jaxpr/cond/branch_1_fun/plq,qk->lpk/dot_general | solution.py:91
  192.0 1.1 broadcast_in_dim.105
  193.1 2.8 fusion.32
  195.9 0.1 broadcast.279
  196.0 25.3 %conditional.3 = (f32[512,8,256]{0,2,1:T(8,128)}) conditional(s32[]{:T(128)} %convert_element_type.117, f32[512,8,256]{0,2,1:T(8,128)} %get-tuple-element.557, (s32[]{:T(128)}, bf16[64,16,256]{2,1,0:T(8,128)(2,1)}, f32[512]{0:T(512)S(1)}, bf16[64,16,512]{2,1,0:T(8,128)(2,1)}, bf16[8,512,512]{2,1,0:T(8,128)(2,1)}, ...), branch_computations={%region_2.2_spmd, %region_3.3_spmd.clone} | conditional | flops 809369600 | bytes 26283966 | solution.py:98
  196.2 0.8 constant_dynamic-slice_fusion.5
  197.0 0.9 constant_dynamic-slice_fusion.3
  198.0 14.6 %multiply_sine_fusion.3 = (f32[8,64,512]{2,1,0:T(8,128)S(1)}, f32[8,64,512]{2,1,0:T(8,128)S(1)}, f32[8,64,512]{2,1,0:T(8,128)S(1)}, f32[8,64,512]{2,1,0:T(8,128)S(1)}) fusion(f32[8,64,512]{2,1,0:T(8,128)S(1)} %get-tuple-element.343, f32[8,64,512]{2,1,0:T(8,128)S(1)} %get-tuple-element.344, f32[8,64,512]{2,1,0:T(8,128)} %get-tuple-element.349, ...), kind=kLoop, calls=%fused_computation.9 | loop fusion | flops 1048576 | bytes 9437184 | tf_op jit(solution)/shard_map/sin | solution.py:32
  212.6 1.0 fusion.8
  213.6 0.2 fusion.2
  213.8 7.5 %bitcast_add_fusion = f32[512,8,256]{0,2,1:T(8,128)} fusion(f32[512,8,256]{0,2,1:T(8,128)} %get-tuple-element.329, bf16[128,256,1]{1,0,2:T(8,128)(2,1)S(1)} %bitcast.39, bf16[8,128,512]{2,1,0:T(8,128)(2,1)S(1)} %fusion.2, bf16[8,512,512]{2,1,0:T(8,128)(2,1)} %get-tuple-element.333), kind=kOutput, calls=%fused_computation.1 | convolution fusion | flops 806879232 | bytes 13697024 | tf_op jit(solution)/shard_map/while/body/eval_jaxpr/cond/branch_1_fun/plq,qk->lpk/dot_general | solution.py:91
  221.3 1.1 broadcast_in_dim.105
  222.4 2.8 fusion.32
  225.3 1.1 broadcast_in_dim.105
  226.4 2.8 fusion.32
  229.4 1.1 broadcast_in_dim.105
  230.5 2.8 fusion.32
  233.5 1.1 broadcast_in_dim.105
  234.6 2.8 fusion.32
  237.5 2.5 convert_bitcast_fusion
  240.0 19.9 %all_to_all.16 = bf16[8,512,1,256]{1,3,2,0:T(8,128)(2,1)S(1)} all-to-all(bf16[8,512,1,256]{1,3,2,0:T(8,128)(2,1)S(1)} %convert_bitcast_fusion), channel_id=1, replica_groups=mesh['row'=8,'col'=32] {'row'}, dimensions={0} | all-to-all | bytes 4194304 | tf_op jit(solution)/shard_map/all_to_all | solution.py:26
  259.9 0.3 bitcast_reduce_fusion
  260.2 0.1 copy.30
  260.3 131.5 %all_to_all.17 = bf16[32,16,1,256]{3,1,2,0:T(8,128)(2,1)S(1)} all-to-all(bf16[32,16,1,256]{3,1,2,0:T(8,128)(2,1)S(1)} %bitcast.40), channel_id=1, replica_groups=mesh['row'=8,'col'=32] {'col'}, dimensions={0} | all-to-all | bytes 524288 | tf_op jit(solution)/shard_map/all_to_all | solution.py:26
  391.8 0.6 reduce_sum.40
  (38 shorter events, 1.6 us)
Async XLA Ops:
  6.5 28.0 %copy-start.1 = (s32[8]{0:T(128)S(1)}, s32[8]{0:T(128)}, u32[]{:S(2)}) copy-start(s32[8]{0:T(128)} %param.11) | copy-start | bytes 100
  6.5 28.4 %copy-start = (bf16[64,16,512]{2,1,0:T(8,128)(2,1)S(1)}, bf16[64,16,512]{2,1,0:T(8,128)(2,1)}, u32[]{:S(2)}) copy-start(bf16[64,16,512]{2,1,0:T(8,128)(2,1)} %param.9) | copy-start | bytes 3145732
  6.5 28.1 %copy-start.2 = (s32[512,2]{0,1:T(2,128)S(1)}, s32[512,2]{0,1:T(2,128)}, u32[]{:S(2)}) copy-start(s32[512,2]{0,1:T(2,128)} %param.12) | copy-start | bytes 12292
  6.5 28.4 %copy-start.3 = (f32[512]{0:T(512)S(1)}, f32[512]{0:T(512)}, u32[]{:S(2)}) copy-start(f32[512]{0:T(512)} %param.13) | copy-start | bytes 6148
  6.5 95.1 %all-gather.2.cloned.1.call-start = ((), (), s32[]{:S(2)}) async-start(), calls=%async_computation.3 | async-start | bytes 4325376 | tf_op jit(solution)/shard_map/all_gather | solution.py:72
Sparse Core Ops, SparseCore 0:
  34.6 66.9 all-gather.1
where the time goes:
time: 400 us; the launch traced here: 399 us
  blocking collectives  175 us (44%)
  other arithmetic  92.4 us (23%)
  waiting for transfers between devices  65.4 us (16%)
  matrix products  32.4 us (8%)
  local copies, waits for them, and re-layouts  20 us (5%)
  between operations  13.5 us (3%)
    all_to_all x2, blocking collectives, summed_on_arrival(): lax.all_to_all(split_up(array, dim, length), axis, 0, 0, tiled=True)  151 us
    all_gather x1, waiting for transfers between devices, per_device(): panel_rows = lax.all_gather(summed, 'col', axis=1, tiled=True)  65.4 us
    sin x4, other arithmetic, mask_coef(): jnp.sin(cell_angle * (wavenumber * span_stop % NPHI).astype(jnp.float32))  58.4 us
    dot_general x4, matrix products, add_terms(): jnp.einsum('plq,qk->lpk', panel_block, vec_block, preferred_element_type=...  29.9 us
    all_to_all x1, blocking collectives, from_everyone(): return lax.all_to_all(copies, axis, split_axis=0, concat_axis=0, tiled=True)  23.6 us
    convert_element_type x8, other arithmetic, mask_coef(): (wavenumber * span_start % NPHI).astype(jnp.float32)  22.5 us
    broadcast_in_dim x8, local copies, waits for them, and re-layouts, mask_coef(): jnp.where(wavenumber == 0, span_width, cell_angle * (upper_sine - lower_s...  8.66 us
  transfers between devices with their start and end apart: 1, of which 1 were waited for; matrix products, arithmetic and copies ran while one was open for 0% of the time, Pallas kernels for 0%

commit v1 on v0

--- a/solution.py
+++ b/solution.py
@@ -69,7 +69,10 @@
         .astype(jnp.float32)
         .astype(jnp.bfloat16)
     )
-    panel_rows = lax.all_gather(summed, "col", axis=1, tiled=True)
+    devices = lax.axis_size("col")
+    blocks = jnp.stack([summed for _ in range(devices)])
+    blocks = lax.all_to_all(blocks, "col", split_axis=0, concat_axis=0)
+    panel_rows = jnp.concatenate(blocks, axis=1)
     mix_coef = cycle_mix(panel_orders, local_orders, cycle_span, cycle_weight)
     order_block = 8
 

time: 400 us -> 429 us (1.073)
  waiting for transfers between devices: 65.4 us -> 92.4 us
  between operations: 13.5 us -> 0.11 us
  starting transfers between devices: 0.03 us -> 10.7 us
  local copies, waits for them, and re-layouts: 20 us -> 27.3 us
    all_to_all x0 -> x1, waiting for transfers between devices: none -> 92.4 us  [per_device(): blocks = lax.all_to_all(blocks, 'col', split_axis=0, concat_axis=0)]
    all_gather x1 -> x0, waiting for transfers between devices: 65.4 us -> none  [per_device(): panel_rows = lax.all_gather(summed, 'col', axis=1, tiled=True)]
    all_to_all x0 -> x1, starting transfers between devices: none -> 10.7 us  [per_device(): blocks = lax.all_to_all(blocks, 'col', split_axis=0, concat_axis=0)]
    all_to_all x0 -> x1, local copies, waits for them, and re-layouts: none -> 4.76 us  [per_device(): blocks = lax.all_to_all(blocks, 'col', split_axis=0, concat_axis=0)]
where the time goes in v1:
time: 429 us; the launch traced here: 428 us
  blocking collectives  173 us (40%)
  waiting for transfers between devices  92.4 us (22%)
  other arithmetic  91.6 us (21%)
  matrix products  32.4 us (8%)
  local copies, waits for them, and re-layouts  27.3 us (6%)
  starting transfers between devices  10.7 us (2%)
    all_to_all x2, blocking collectives, summed_on_arrival(): lax.all_to_all(split_up(array, dim, length), axis, 0, 0, tiled=True)  149 us
    all_to_all x1, waiting for transfers between devices, per_device(): blocks = lax.all_to_all(blocks, 'col', split_axis=0, concat_axis=0)  92.4 us
    sin x4, other arithmetic, mask_coef(): jnp.sin(cell_angle * (wavenumber * span_stop % NPHI).astype(jnp.float32))  58.4 us
    dot_general x4, matrix products, add_terms(): jnp.einsum('plq,qk->lpk', panel_block, vec_block, preferred_element_type=...  29.9 us
    all_to_all x1, blocking collectives, from_everyone(): return lax.all_to_all(copies, axis, split_axis=0, concat_axis=0, tiled=True)  23.6 us
    convert_element_type x8, other arithmetic, mask_coef(): (wavenumber * span_start % NPHI).astype(jnp.float32)  22.4 us
    all_to_all x1, starting transfers between devices, per_device(): blocks = lax.all_to_all(blocks, 'col', split_axis=0, concat_axis=0)  10.7 us
    broadcast_in_dim x8, local copies, waits for them, and re-layouts, mask_coef(): jnp.where(wavenumber == 0, span_width, cell_angle * (upper_sine - lower_s...  8.69 us
  transfers between devices with their start and end apart: 1, of which 1 were waited for; matrix products, arithmetic and copies ran while one was open for 0% of the time, Pallas kernels for 0%

profile of v1, /device:TPU:1, one launch (start us, length us, event | category | flops | bytes accessed | tf_op | source)
XLA Modules:
  0.0 428.1 jit_solution(6770281893427655529)
XLA Ops:
  0.0 0.7 broadcast_compare_fusion.1
  0.7 2.5 fusion.20
  3.2 0.1 broadcast_in_dim.79
  3.4 23.6 %all_to_all.20 = bf16[8,8,16,512]{3,2,1,0:T(8,128)(2,1)S(1)} all-to-all(bf16[8,8,16,512]{3,2,1,0:T(8,128)(2,1)S(1)} %broadcast_in_dim.79), channel_id=1, replica_groups=mesh['row'=8,'col'=32] {'row'}, dimensions={0} | all-to-all | bytes 2097152 | tf_op jit(solution)/shard_map/all_to_all | solution.py:12
  27.0 0.2 reduce_sum.38
  27.2 2.5 stack.2
  29.7 10.7 %all-to-all-start.1 = ((bf16[32,8,16,512]{3,2,1,0:T(8,128)(2,1)}), bf16[32,8,16,512]{3,2,1,0:T(8,128)(2,1)}, u32[]{:S(2)}, u32[]{:S(2)}) async-start(bf16[32,8,16,512]{3,2,1,0:T(8,128)(2,1)} %stack.2), calls=%async_computation.1 | async-start | bytes 8388608 | tf_op jit(solution)/shard_map/all_to_all | solution.py:74
  40.7 0.1 multiply_select_fusion.4
  40.8 1.3 broadcast_select_fusion
  42.1 92.4 %all-to-all-done.1 = bf16[32,8,16,512]{3,2,1,0:T(8,128)(2,1)} async-done(((bf16[32,8,16,512]{3,2,1,0:T(8,128)(2,1)}), bf16[32,8,16,512]{3,2,1,0:T(8,128)(2,1)}, u32[]{:S(2)}, u32[]{:S(2)}) %all-to-all-start.1) | async-done | bytes 4194336 | tf_op jit(solution)/shard_map/all_to_all | solution.py:74
  134.5 4.8 %copy.30 = bf16[32,8,16,512]{3,2,0,1:T(8,128)(2,1)} copy(bf16[32,8,16,512]{3,2,1,0:T(8,128)(2,1)} %all-to-all-done.1) | data formatting | bytes 8388608 | tf_op jit(solution)/shard_map/all_to_all | solution.py:74
  139.2 2.5 broadcast_in_dim.71
  141.7 133.3 %while.19 = (s32[]{:T(128)}, f32[512,8,256]{0,2,1:T(8,128)}, s32[]{:T(128)}, s32[]{:T(128)}, bf16[64,16,256]{2,1,0:T(8,128)(2,1)}, /*index=5*/bf16[64,16,512]{2,...) while((s32[]{:T(128)}, f32[512,8,256]{0,2,1:T(8,128)}, ...), condition=%wide.region_4.5_spmd.clone, body=%wide.region_1.4_spmd.clone.sunk | while | flops 823001088 | bytes 32586012 | solution.py:104
  141.7 1.1 broadcast_in_dim.105
  142.8 2.8 fusion.32
  145.6 0.1 broadcast.281
  145.8 25.3 %conditional.3 = (f32[512,8,256]{0,2,1:T(8,128)}) conditional(s32[]{:T(128)} %convert_element_type.117, f32[512,8,256]{0,2,1:T(8,128)} %get-tuple-element.557, (s32[]{:T(128)}, bf16[64,16,256]{2,1,0:T(8,128)(2,1)}, f32[512]{0:T(512)S(1)}, bf16[64,16,512]{2,1,0:T(8,128)(2,1)}, bf16[8,512,512]{2,1,0:T(8,128)(2,1)}, ...), branch_computations={%region_2.2_spmd, %region_3.3_spmd.clone} | conditional | flops 809369600 | bytes 26283966 | solution.py:101
  145.9 0.8 constant_dynamic-slice_fusion.5
  146.8 0.9 constant_dynamic-slice_fusion.3
  147.7 14.6 %multiply_sine_fusion.3 = (f32[8,64,512]{2,1,0:T(8,128)S(1)}, f32[8,64,512]{2,1,0:T(8,128)S(1)}, f32[8,64,512]{2,1,0:T(8,128)S(1)}, f32[8,64,512]{2,1,0:T(8,128)S(1)}) fusion(f32[8,64,512]{2,1,0:T(8,128)S(1)} %get-tuple-element.343, f32[8,64,512]{2,1,0:T(8,128)S(1)} %get-tuple-element.344, f32[8,64,512]{2,1,0:T(8,128)} %get-tuple-element.349, ...), kind=kLoop, calls=%fused_computation.9 | loop fusion | flops 1048576 | bytes 9437184 | tf_op jit(solution)/shard_map/sin | solution.py:32
  162.3 1.0 fusion.8
  163.4 0.2 fusion.2
  163.5 7.5 %bitcast_add_fusion = f32[512,8,256]{0,2,1:T(8,128)} fusion(f32[512,8,256]{0,2,1:T(8,128)} %get-tuple-element.329, bf16[128,256,1]{1,0,2:T(8,128)(2,1)S(1)} %bitcast.43, bf16[8,128,512]{2,1,0:T(8,128)(2,1)S(1)} %fusion.2, bf16[8,512,512]{2,1,0:T(8,128)(2,1)} %get-tuple-element.333), kind=kOutput, calls=%fused_computation.1 | convolution fusion | flops 806879232 | bytes 13697024 | tf_op jit(solution)/shard_map/while/body/eval_jaxpr/cond/branch_1_fun/plq,qk->lpk/dot_general | solution.py:94
  171.0 1.1 broadcast_in_dim.105
  172.1 2.8 fusion.32
  175.0 25.3 %conditional.3 = (f32[512,8,256]{0,2,1:T(8,128)}) conditional(s32[]{:T(128)} %convert_element_type.117, f32[512,8,256]{0,2,1:T(8,128)} %get-tuple-element.557, (s32[]{:T(128)}, bf16[64,16,256]{2,1,0:T(8,128)(2,1)}, f32[512]{0:T(512)S(1)}, bf16[64,16,512]{2,1,0:T(8,128)(2,1)}, bf16[8,512,512]{2,1,0:T(8,128)(2,1)}, ...), branch_computations={%region_2.2_spmd, %region_3.3_spmd.clone} | conditional | flops 809369600 | bytes 26283966 | solution.py:101
  175.2 0.8 constant_dynamic-slice_fusion.5
  176.1 0.9 constant_dynamic-slice_fusion.3
  177.0 14.6 %multiply_sine_fusion.3 = (f32[8,64,512]{2,1,0:T(8,128)S(1)}, f32[8,64,512]{2,1,0:T(8,128)S(1)}, f32[8,64,512]{2,1,0:T(8,128)S(1)}, f32[8,64,512]{2,1,0:T(8,128)S(1)}) fusion(f32[8,64,512]{2,1,0:T(8,128)S(1)} %get-tuple-element.343, f32[8,64,512]{2,1,0:T(8,128)S(1)} %get-tuple-element.344, f32[8,64,512]{2,1,0:T(8,128)} %get-tuple-element.349, ...), kind=kLoop, calls=%fused_computation.9 | loop fusion | flops 1048576 | bytes 9437184 | tf_op jit(solution)/shard_map/sin | solution.py:32
  191.6 1.0 fusion.8
  192.7 0.2 fusion.2
  192.8 7.5 %bitcast_add_fusion = f32[512,8,256]{0,2,1:T(8,128)} fusion(f32[512,8,256]{0,2,1:T(8,128)} %get-tuple-element.329, bf16[128,256,1]{1,0,2:T(8,128)(2,1)S(1)} %bitcast.43, bf16[8,128,512]{2,1,0:T(8,128)(2,1)S(1)} %fusion.2, bf16[8,512,512]{2,1,0:T(8,128)(2,1)} %get-tuple-element.333), kind=kOutput, calls=%fused_computation.1 | convolution fusion | flops 806879232 | bytes 13697024 | tf_op jit(solution)/shard_map/while/body/eval_jaxpr/cond/branch_1_fun/plq,qk->lpk/dot_general | solution.py:94
  200.3 1.1 broadcast_in_dim.105
  201.4 2.8 fusion.32
  204.3 25.3 %conditional.3 = (f32[512,8,256]{0,2,1:T(8,128)}) conditional(s32[]{:T(128)} %convert_element_type.117, f32[512,8,256]{0,2,1:T(8,128)} %get-tuple-element.557, (s32[]{:T(128)}, bf16[64,16,256]{2,1,0:T(8,128)(2,1)}, f32[512]{0:T(512)S(1)}, bf16[64,16,512]{2,1,0:T(8,128)(2,1)}, bf16[8,512,512]{2,1,0:T(8,128)(2,1)}, ...), branch_computations={%region_2.2_spmd, %region_3.3_spmd.clone} | conditional | flops 809369600 | bytes 26283966 | solution.py:101
  204.5 0.8 constant_dynamic-slice_fusion.5
  205.3 0.9 constant_dynamic-slice_fusion.3
  206.3 14.6 %multiply_sine_fusion.3 = (f32[8,64,512]{2,1,0:T(8,128)S(1)}, f32[8,64,512]{2,1,0:T(8,128)S(1)}, f32[8,64,512]{2,1,0:T(8,128)S(1)}, f32[8,64,512]{2,1,0:T(8,128)S(1)}) fusion(f32[8,64,512]{2,1,0:T(8,128)S(1)} %get-tuple-element.343, f32[8,64,512]{2,1,0:T(8,128)S(1)} %get-tuple-element.344, f32[8,64,512]{2,1,0:T(8,128)} %get-tuple-element.349, ...), kind=kLoop, calls=%fused_computation.9 | loop fusion | flops 1048576 | bytes 9437184 | tf_op jit(solution)/shard_map/sin | solution.py:32
  220.9 1.0 fusion.8
  221.9 0.2 fusion.2
  222.1 7.5 %bitcast_add_fusion = f32[512,8,256]{0,2,1:T(8,128)} fusion(f32[512,8,256]{0,2,1:T(8,128)} %get-tuple-element.329, bf16[128,256,1]{1,0,2:T(8,128)(2,1)S(1)} %bitcast.43, bf16[8,128,512]{2,1,0:T(8,128)(2,1)S(1)} %fusion.2, bf16[8,512,512]{2,1,0:T(8,128)(2,1)} %get-tuple-element.333), kind=kOutput, calls=%fused_computation.1 | convolution fusion | flops 806879232 | bytes 13697024 | tf_op jit(solution)/shard_map/while/body/eval_jaxpr/cond/branch_1_fun/plq,qk->lpk/dot_general | solution.py:94
  229.6 1.1 broadcast_in_dim.105
  230.7 2.8 fusion.32
  233.6 25.3 %conditional.3 = (f32[512,8,256]{0,2,1:T(8,128)}) conditional(s32[]{:T(128)} %convert_element_type.117, f32[512,8,256]{0,2,1:T(8,128)} %get-tuple-element.557, (s32[]{:T(128)}, bf16[64,16,256]{2,1,0:T(8,128)(2,1)}, f32[512]{0:T(512)S(1)}, bf16[64,16,512]{2,1,0:T(8,128)(2,1)}, bf16[8,512,512]{2,1,0:T(8,128)(2,1)}, ...), branch_computations={%region_2.2_spmd, %region_3.3_spmd.clone} | conditional | flops 809369600 | bytes 26283966 | solution.py:101
  233.8 0.8 constant_dynamic-slice_fusion.5
  234.6 0.9 constant_dynamic-slice_fusion.3
  235.6 14.6 %multiply_sine_fusion.3 = (f32[8,64,512]{2,1,0:T(8,128)S(1)}, f32[8,64,512]{2,1,0:T(8,128)S(1)}, f32[8,64,512]{2,1,0:T(8,128)S(1)}, f32[8,64,512]{2,1,0:T(8,128)S(1)}) fusion(f32[8,64,512]{2,1,0:T(8,128)S(1)} %get-tuple-element.343, f32[8,64,512]{2,1,0:T(8,128)S(1)} %get-tuple-element.344, f32[8,64,512]{2,1,0:T(8,128)} %get-tuple-element.349, ...), kind=kLoop, calls=%fused_computation.9 | loop fusion | flops 1048576 | bytes 9437184 | tf_op jit(solution)/shard_map/sin | solution.py:32
  250.2 1.0 fusion.8
  251.2 0.2 fusion.2
  251.4 7.5 %bitcast_add_fusion = f32[512,8,256]{0,2,1:T(8,128)} fusion(f32[512,8,256]{0,2,1:T(8,128)} %get-tuple-element.329, bf16[128,256,1]{1,0,2:T(8,128)(2,1)S(1)} %bitcast.43, bf16[8,128,512]{2,1,0:T(8,128)(2,1)S(1)} %fusion.2, bf16[8,512,512]{2,1,0:T(8,128)(2,1)} %get-tuple-element.333), kind=kOutput, calls=%fused_computation.1 | convolution fusion | flops 806879232 | bytes 13697024 | tf_op jit(solution)/shard_map/while/body/eval_jaxpr/cond/branch_1_fun/plq,qk->lpk/dot_general | solution.py:94
  258.9 1.1 broadcast_in_dim.105
  260.0 2.8 fusion.32
  262.9 1.1 broadcast_in_dim.105
  264.0 2.8 fusion.32
  267.0 1.1 broadcast_in_dim.105
  268.1 2.8 fusion.32
  271.0 1.1 broadcast_in_dim.105
  272.1 2.8 fusion.32
  275.1 2.5 convert_bitcast_fusion
  277.5 19.9 %all_to_all.21 = bf16[8,512,1,256]{1,3,2,0:T(8,128)(2,1)S(1)} all-to-all(bf16[8,512,1,256]{1,3,2,0:T(8,128)(2,1)S(1)} %convert_bitcast_fusion), channel_id=1, replica_groups=mesh['row'=8,'col'=32] {'row'}, dimensions={0} | all-to-all | bytes 4194304 | tf_op jit(solution)/shard_map/all_to_all | solution.py:26
  297.5 0.3 bitcast_reduce_fusion
  297.8 0.1 copy.32
  297.9 129.5 %all_to_all.22 = bf16[32,16,1,256]{3,1,2,0:T(8,128)(2,1)S(1)} all-to-all(bf16[32,16,1,256]{3,1,2,0:T(8,128)(2,1)S(1)} %bitcast.44), channel_id=1, replica_groups=mesh['row'=8,'col'=32] {'col'}, dimensions={0} | all-to-all | bytes 524288 | tf_op jit(solution)/shard_map/all_to_all | solution.py:26
  427.4 0.6 reduce_sum.40
  (39 shorter events, 1.9 us)
Async XLA Ops:
  29.6 10.8 %copy-start.1 = (s32[8]{0:T(128)S(1)}, s32[8]{0:T(128)}, u32[]{:S(2)}) copy-start(s32[8]{0:T(128)} %param.11) | copy-start | bytes 100
  29.6 10.8 %copy-start.2 = (s32[512,2]{0,1:T(2,128)S(1)}, s32[512,2]{0,1:T(2,128)}, u32[]{:S(2)}) copy-start(s32[512,2]{0,1:T(2,128)} %param.12) | copy-start | bytes 12292
  29.6 11.1 %copy-start.3 = (f32[512]{0:T(512)S(1)}, f32[512]{0:T(512)}, u32[]{:S(2)}) copy-start(f32[512]{0:T(512)} %param.13) | copy-start | bytes 6148
  29.7 11.2 %copy-start = (bf16[64,16,512]{2,1,0:T(8,128)(2,1)S(1)}, bf16[64,16,512]{2,1,0:T(8,128)(2,1)}, u32[]{:S(2)}) copy-start(bf16[64,16,512]{2,1,0:T(8,128)(2,1)} %param.9) | copy-start | bytes 3145732
  29.7 104.8 %all-to-all-start.1 = ((bf16[32,8,16,512]{3,2,1,0:T(8,128)(2,1)}), bf16[32,8,16,512]{3,2,1,0:T(8,128)(2,1)}, u32[]{:S(2)}, u32[]{:S(2)}) async-start(bf16[32,8,16,512]{3,2,1,0:T(8,128)(2,1)} %stack.2), calls=%async_computation.1 | async-start | bytes 8388608 | tf_op jit(solution)/shard_map/all_to_all | solution.py:74
